TPU v7x, 32 devices: a whole 2x2x4 slice. The times are simulated.
32 devices in a mesh: blk: 16 (over z, y, core), head: 2 (over x).
Axes of the slice: x: 2, y: 2, z: 4, core: 2. Of those that a mesh axis runs over, the one named last changes fastest.
Arguments:
- query_nope: bfloat16 [1024, 8192], P('blk', 'head'), may hold values from -140 to 140
- query_rope: bfloat16 [1024, 4096], P('blk', 'head'), may hold values from -6 to 6
- compressed: bfloat16 [1024, 576], P(('blk', 'head')), may hold values from -6 to 6
- latent_gain: float32 [512], replicated, may hold values from 0.1 to 1.9
- key_up: bfloat16 [64, 128, 512], P('head'), may hold values from -0.5 to 0.5
- value_up: bfloat16 [64, 512, 128], P('head'), may hold values from -1.5 to 1.5
- span_order: int32 [32], replicated, may hold values from 0 to 31, each once
Outputs:
- attended: bfloat16 [1024, 8192], P('blk', 'head')
Inputs may be any that keep to these rules, and one draw needn't show every extreme that they name: Every number appears once; device index i of blk holds the blocks span_order[2 i] and span_order[2 i + 1].
All inputs are finite; a program needn't handle non-finite values.
Results may differ from a plain program's by a relative error of at most 0.0075.
The roundings to bfloat16 on the way count: a program that leaves them out, or rounds other values in their place, can miss the bound.
Values may be sent and summed in bfloat16 or wider, within the bound.
A program may use at most 64 MiB of HBM per device.

v0:
```python
import jax
import jax.numpy as jnp
from jax import lax
from jax.sharding import PartitionSpec as P

norm_epsilon = 1e-06
rope_base = 10000.0
masked_score = -1e30


def lookup(entries, index_array):
    slots = jnp.arange(entries.shape[0], dtype=jnp.int32)
    matches = index_array[..., None] == slots
    return jnp.sum(jnp.where(matches, entries, 0), axis=-1)


def rotate(values, positions):
    half_width = values.shape[-1] // 2
    frequency = rope_base ** (-jnp.arange(half_width, dtype=jnp.float32) / half_width)
    angles = positions.astype(jnp.float32)[..., None] * frequency
    cosine = jnp.cos(angles)
    sine_value = jnp.sin(angles)
    leading = values[..., :half_width]
    trailing = values[..., half_width:]
    return jnp.concatenate(
        [leading * cosine - trailing * sine_value, leading * sine_value + trailing * cosine],
        axis=-1,
    )


def shards(query_nope, query_rope, compressed, latent_gain, key_up, value_up, span_order):
    tokens_here = query_nope.shape[0]
    heads_here = key_up.shape[0]
    nope_width = key_up.shape[1]
    latent_width = key_up.shape[2]
    rope_width = query_rope.shape[1] // heads_here
    value_width = value_up.shape[2]
    half_block = tokens_here // 2
    slice_count = compressed.shape[0]
    block_id = lax.axis_index("blk")
    head_id = lax.axis_index("head")

    def positions_of(row_ids):
        return lookup(span_order, row_ids // half_block) * half_block + row_ids % half_block

    query_pos = positions_of(block_id * tokens_here + jnp.arange(tokens_here, dtype=jnp.int32))
    own_rows = (
        block_id * tokens_here + head_id * slice_count + jnp.arange(slice_count, dtype=jnp.int32)
    )
    own_pos = positions_of(own_rows)
    latent = compressed[:, :latent_width].astype(jnp.float32)
    latent = (
        latent
        * lax.rsqrt(jnp.mean(latent * latent, axis=1, keepdims=True) + norm_epsilon)
        * latent_gain
    )
    latent = latent.astype(jnp.bfloat16)
    key_rot = rotate(compressed[:, latent_width:].astype(jnp.float32), own_pos).astype(jnp.bfloat16)
    key_rows = jnp.concatenate([latent, key_rot], axis=1)
    nope_parts = query_nope.reshape(tokens_here, heads_here, nope_width)
    query_lat = jnp.einsum(
        "thn,hnl->thl", nope_parts, key_up, preferred_element_type=jnp.float32
    ).astype(jnp.bfloat16)
    query_rot = rotate(
        query_rope.reshape(tokens_here, heads_here, rope_width).astype(jnp.float32),
        query_pos[:, None],
    ).astype(jnp.bfloat16)
    row_count = tokens_here * heads_here
    queries = jnp.concatenate([query_lat, query_rot], axis=2).reshape(
        row_count, latent_width + rope_width
    )
    query_rows_pos = jnp.repeat(query_pos, heads_here)
    score_scale = (nope_width + rope_width) ** (-0.5)
    block_keys = lax.all_gather(key_rows, "head", axis=0, tiled=True)
    shard_keys = lax.all_gather(block_keys, "blk", axis=0, tiled=True)
    row_ids = jnp.arange(shard_keys.shape[0], dtype=jnp.int32)
    run_max = jnp.full((row_count,), masked_score, jnp.float32)
    scores = (
        jnp.einsum("qd,kd->qk", queries, shard_keys, preferred_element_type=jnp.float32)
        * score_scale
    )
    visible = positions_of(row_ids)[None, :] <= query_rows_pos[:, None]
    scores = jnp.where(visible, scores, masked_score)
    new_max = jnp.maximum(run_max, jnp.max(scores, axis=1))
    weight = jnp.where(visible, jnp.exp(scores - new_max[:, None]), 0.0)
    new_sum = jnp.sum(weight, axis=1)
    product = jnp.dot(
        weight.astype(jnp.bfloat16),
        shard_keys[:, :latent_width],
        preferred_element_type=jnp.float32,
    )
    folded = (new_max, new_sum, product)
    run_max, run_sum, run_acc = folded
    lat_out = (
        (run_acc / run_sum[:, None])
        .astype(jnp.bfloat16)
        .reshape(tokens_here, heads_here, latent_width)
    )
    attended = jnp.einsum(
        "thl,hlv->thv", lat_out, value_up, preferred_element_type=jnp.float32
    ).astype(jnp.bfloat16)
    return attended.reshape(tokens_here, heads_here * value_width)


def solution(mesh):
    in_specs = (
        P("blk", "head"),
        P("blk", "head"),
        P(("blk", "head"), None),
        P(),
        P("head", None, None),
        P("head", None, None),
        P(),
    )
    out_specs = P("blk", "head")
    return jax.shard_map(shards, mesh=mesh, in_specs=in_specs, out_specs=out_specs, check_vma=False)
```

profile of v0, /device:TPU:1, one launch (start us, length us, event | category | flops | bytes accessed | tf_op | source)
XLA Modules:
  0.0 77.7 jit_solution(14785605622629866800)
XLA Ops:
  6.5 0.0 copy-start
  6.5 0.0 all-gather.2.cloned.1.call-start
  6.6 0.9 %fusion.19 = f32[32]{0:T(128)S(1)} fusion(bf16[32,576]{1,0:T(8,128)(2,1)} %param.9), kind=kLoop, calls=%fused_computation.24 | loop fusion | flops 49120 | bytes 32896 | tf_op jit(solution)/shard_map/reduce_sum | solution.py:54
  7.5 0.7 slice_convert_fusion
  8.2 0.8 %select_reduce_fusion.1 = s32[32]{0:T(128)S(1)} fusion(s32[32]{0:T(128)} %param.13, s32[32]{0:T(128)S(1)} %and_select_fusion.1), kind=kLoop, calls=%fused_computation.40 | loop fusion | flops 3040 | bytes 384 | tf_op jit(solution)/shard_map/reduce_sum | solution.py:14
  9.1 0.9 %fusion.21 = bf16[32,512]{1,0:T(8,128)(2,1)S(1)} fusion(f32[512]{0:T(512)} %param.10, f32[32]{0:T(128)S(1)} %add_rsqrt_fusion, bf16[32,576]{1,0:T(8,128)(2,1)} %param.9), kind=kLoop, calls=%fused_computation.26 | loop fusion | flops 65536 | bytes 67712 | tf_op jit(solution)/shard_map/convert_element_type | solution.py:57
  9.9 0.1 fusion.27
  10.1 0.1 pad_maximum_fusion.1
  10.1 4.2 %all_gather.6 = bf16[64,576]{1,0:T(8,128)(2,1)} all-gather(bf16[32,576]{1,0:T(8,128)(2,1)S(1)} %pad_maximum_fusion.1), channel_id=1, replica_groups=mesh['blk'=16,'head'=2] {'head'}, dimensions={0}, use_global_device_ids=true | all-gather | bytes 110592 | tf_op jit(solution)/shard_map/all_gather | solution.py:74
  14.3 0.0 all-gather.2.cloned.1.call-update
  14.3 0.7 select_reduce_fusion.2
  15.1 0.1 broadcast_in_dim.57
  15.2 0.1 le.16
  15.3 1.4 %reshape.208 = f32[64,32,64]{2,1,0:T(8,128)S(1)} reshape(bf16[64,2048]{1,0:T(8,128)(2,1)} %param.8) | data formatting | bytes 786432 | tf_op jit(solution)/shard_map/convert_element_type | solution.py:65
  16.6 0.0 copy-start.1
  16.6 0.2 multiply_cosine_fusion
  16.8 0.4 fusion.46
  17.2 1.2 %subtract_convert_fusion = (bf16[64,32,32]{2,0,1:T(8,128)(2,1)S(1)}, bf16[64,32,32]{2,0,1:T(8,128)(2,1)S(1)}) fusion(f32[64,32,32]{2,1,0:T(8,128)S(1)} %get-tuple-element.10, f32[64,32,32]{2,1,0:T(8,128)S(1)} %get-tuple-element.9, f32[64,32]{1,0:T(8,128)S(1)} %get-tuple-element.14, f32[64,32]{1,0:T(8,128)S(1)} %get-tuple-element.13), kind=kLoop, calls=%fused_computation.16 | loop fusion | flops 524288 | bytes 802816 | tf_op jit(solution)/shard_map/convert.3
  18.4 0.0 copy-done
  18.4 0.4 copy-done.1
  18.8 0.7 convert_bitcast_fusion
  19.5 0.0 copy-start.3
  19.6 0.5 pad_maximum_fusion
  20.1 1.5 %copy.19 = bf16[64,32,576]{2,1,0:T(8,128)(2,1)S(1)} copy(bf16[64,32,576]{2,0,1:T(8,128)(2,1)S(1)} %pad_maximum_fusion) | data formatting | bytes 4718592 | tf_op jit(solution)/shard_map/concatenate | solution.py:69
  21.6 0.1 select_reduce_fusion
  21.7 34.5 %all-gather.2.cloned.1.call-done = bf16[1024,576]{1,0:T(8,128)(2,1)} async-done(((bf16[64,576]{1,0:T(8,128)(2,1)}), bf16[1024,576]{1,0:T(8,128)(2,1)}) %all-gather.2.cloned.1.call-update) | async-done | bytes 1179664 | tf_op jit(solution)/shard_map/all_gather | solution.py:75
  56.2 4.9 %fusion = (f32[2048]{0:T(1024)S(1)}, f32[2048,1024]{0,1:T(8,128)S(1)}) fusion(s32[2048]{0:T(1024)S(1)} %le.16, s32[1024]{0:T(1024)S(1)} %fusion.36, bf16[2048,576]{1,0:T(8,128)(2,1)S(1)} %bitcast.21, bf16[1024,576]{1,0:T(8,128)(2,1)} %all-gather.2.cloned.1.call-done), kind=kOutput, calls=%fused_computation.2 | convolution fusion | flops 2424305664 | bytes 11948032 | tf_op jit(solution)/shard_map/qd,kd->qk/dot_general | solution.py:79
  61.1 2.9 %fusion.1 = f32[2048]{0:T(1024)S(1)} fusion(f32[2048,1024]{0,1:T(8,128)S(1)} %get-tuple-element.16, f32[2048]{0:T(1024)S(1)} %broadcast_maximum_fusion, s32[2048]{0:T(1024)S(1)} %le.16, s32[1024]{0:T(1024)S(1)} %fusion.36), kind=kLoop, calls=%fused_computation.3 | loop fusion | flops 12580864 | bytes 8417280 | tf_op jit(solution)/shard_map/reduce_sum | solution.py:86
  64.0 0.0 copy-start.2
  64.0 3.5 %divide_convert_fusion = bf16[2048,512]{1,0:T(8,128)(2,1)S(1)} fusion(f32[2048]{0:T(1024)S(1)} %fusion.1, f32[2048,1024]{0,1:T(8,128)S(1)} %get-tuple-element.16, f32[2048]{0:T(1024)S(1)} %broadcast_maximum_fusion, s32[2048]{0:T(1024)S(1)} %le.16, s32[1024]{0:T(1024)S(1)} %fusion.36, bf16[1024,576]{1,0:T(8,128)(2,1)S(1)} %copy-done.4), kind=kOutput, calls=%fused_computation.5 | convolution fusion | flops 2162163712 | bytes 11563008 | tf_op jit(solution)/shard_map/dot_general | solution.py:87
  67.5 2.5 %fusion.13 = bf16[32,8,8,128]{3,2,1,0:T(8,128)(2,1)S(1)} fusion(bf16[32,512,128]{2,1,0:T(8,128)(2,1)S(1)} %copy-done.2, bf16[64,32,512]{2,1,0:T(8,128)(2,1)S(1)} %bitcast.22), kind=kOutput, calls=%fused_computation.13 | convolution fusion | flops 268697600 | bytes 6815744 | tf_op jit(solution)/shard_map/thl,hlv->thv/dot_general | solution.py:99
  70.0 0.9 %copy.41 = bf16[32,8,8,128]{3,2,0,1:T(8,128)(2,1)} copy(bf16[32,8,8,128]{3,2,1,0:T(8,128)(2,1)S(1)} %fusion.13) | data formatting | bytes 1048576 | tf_op jit(solution)/shard_map/reshape | solution.py:102
  (13 shorter events, 0.1 us)
Async XLA Ops:
  6.5 11.9 %copy-start = (bf16[64,4096]{1,0:T(8,128)(2,1)S(1)}, bf16[64,4096]{1,0:T(8,128)(2,1)}, u32[]{:S(2)}) copy-start(bf16[64,4096]{1,0:T(8,128)(2,1)} %param.7) | copy-start | bytes 1572868
  6.5 49.6 %all-gather.2.cloned.1.call-start = ((), (), s32[]{:S(2)}) async-start(), calls=%async_computation | async-start | bytes 1392640 | tf_op jit(solution)/shard_map/all_gather | solution.py:75
  16.6 2.2 %copy-start.1 = (bf16[32,128,512]{2,1,0:T(8,128)(2,1)S(1)}, bf16[32,128,512]{2,1,0:T(8,128)(2,1)}, u32[]{:S(2)}) copy-start(bf16[32,128,512]{2,1,0:T(8,128)(2,1)} %param.11) | copy-start | bytes 12582916
  19.5 2.0 %copy-start.3 = (s32[32]{0:T(128)S(1)}, s32[32]{0:T(128)}, u32[]{:S(2)}) copy-start(s32[32]{0:T(128)} %param.13) | copy-start | bytes 388
  61.1 2.9 %copy-start.4 = (bf16[1024,576]{1,0:T(8,128)(2,1)S(1)}, bf16[1024,576]{1,0:T(8,128)(2,1)}, u32[]{:S(2)}) copy-start(bf16[1024,576]{1,0:T(8,128)(2,1)} %all-gather.2.cloned.1.call-done) | copy-start | bytes 3538948
  64.0 3.5 %copy-start.2 = (bf16[32,512,128]{2,1,0:T(8,128)(2,1)S(1)}, bf16[32,512,128]{2,1,0:T(8,128)(2,1)}, u32[]{:S(2)}) copy-start(bf16[32,512,128]{2,1,0:T(8,128)(2,1)} %param.12) | copy-start | bytes 12582916
Sparse Core Ops, SparseCore 0:
  14.5 41.6 all-gather.1
where the time goes:
time: 78.4 us; the launch traced here: 77.7 us
  waiting for transfers between devices  34.5 us (44%)
  between operations  13.6 us (17%)
  matrix products  11.6 us (15%)
  other arithmetic  9.23 us (12%)
  local copies, waits for them, and re-layouts  4.67 us (6%)
  blocking collectives  4.17 us (5%)
    all_gather x1, waiting for transfers between devices, shards(): shard_keys = lax.all_gather(block_keys, 'blk', axis=0, tiled=True)  34.5 us
    dot_general x1, matrix products, shards(): jnp.einsum('qd,kd->qk', queries, shard_keys, preferred_element_type=jnp.f...  4.93 us
    all_gather x1, blocking collectives, shards(): block_keys = lax.all_gather(key_rows, 'head', axis=0, tiled=True)  4.17 us
    dot_general x1, matrix products, shards(): jnp.dot(weight.astype(jnp.bfloat16), shard_keys[:, :latent_width], prefer...  3.46 us
    reduce_sum x1, other arithmetic, shards(): new_sum = jnp.sum(weight, axis=1)  2.85 us
    dot_general x1, matrix products, shards(): jnp.einsum('thl,hlv->thv', lat_out, value_up, preferred_element_type=jnp....  2.52 us
    reduce_sum x3, other arithmetic, lookup(): return jnp.sum(jnp.where(matches, entries, 0), axis=-1)  1.67 us
  transfers between devices with their start and end apart: 1, of which 1 were waited for; matrix products, arithmetic and copies ran while one was open for 9% of the time, Pallas kernels for 0%

commit v1 on v0

v1 whole, which is shorter than its diff:
```python
import functools
import math

import jax
import jax.numpy as jnp
import numpy as np
from jax import lax
from jax.experimental import pallas as pl
from jax.experimental.pallas import tpu as pltpu
from jax.sharding import PartitionSpec as P

norm_epsilon = 1e-06
rope_base = 10000.0
masked_score = -1e30
LANES = 128
GROUP = 8
MESH = pl.DeviceIdType.MESH


def rotate_tile(tile, cosine, signed_sine, rope_width):
    half = rope_width // 2
    width = tile.shape[-1]
    lane = lax.broadcasted_iota(jnp.int32, tile.shape, 1)
    partner = jnp.where(
        lane % rope_width < half,
        pltpu.roll(tile, width - half, 1),
        pltpu.roll(tile, half, 1),
    )
    return tile * cosine + partner * signed_sine


def angles_of(positions, freq, rope_width):
    angles = positions.astype(jnp.float32) * freq
    lane = lax.broadcasted_iota(jnp.int32, angles.shape, 1)
    sine = jnp.sin(angles)
    return jnp.cos(angles), jnp.where(lane % rope_width < rope_width // 2, -sine, sine)


def body(
    dims,
    remote,
    span_ref,
    keys_in_ref,
    gain_ref,
    freq_ref,
    nope_hbm,
    rope_hbm,
    key_up_hbm,
    value_up_hbm,
    out_hbm,
    nope_ref,
    rope_ref,
    key_up_ref,
    value_up_ref,
    out_ref,
    keys_ref,
    query_ref,
    mask_ref,
    load_sem,
    out_sem,
    send_sem,
    recv_sem,
):
    tokens, heads, nope, latent, rope, value, total, slices = dims
    half_block = tokens // 2
    scale = (nope + rope) ** (-0.5) * math.log2(math.e)
    blk = lax.axis_index("blk")
    head = lax.axis_index("head")
    loads = [
        pltpu.make_async_copy(nope_hbm, nope_ref, load_sem.at[0]),
        pltpu.make_async_copy(rope_hbm, rope_ref, load_sem.at[1]),
        pltpu.make_async_copy(key_up_hbm, key_up_ref, load_sem.at[2]),
        pltpu.make_async_copy(value_up_hbm, value_up_ref, load_sem.at[3]),
    ]
    for load in loads:
        load.start()

    sends = []
    if remote:
        outer = lax.axis_size("blk") // 4
        o, i, c = blk // 4, (blk // 2) % 2, blk % 2

        def device(o_, i_, c_, h_):
            return ((o_ * 2 + i_) * 2 + c_, h_)

        def slot(o_, i_, c_, h_):
            return ((o_ * 2 + i_) * 2 + c_) * 2 + h_

        def block_at(index):
            return keys_ref.at[pl.ds(pl.multiple_of(index * slices, slices), slices)]

        def send(index, target):
            copy = pltpu.make_async_remote_copy(
                src_ref=block_at(index),
                dst_ref=block_at(index),
                send_sem=send_sem.at[len(sends)],
                recv_sem=recv_sem.at[index],
                device_id=target,
                device_id_type=MESH,
            )
            copy.start()
            sends.append(copy)

        def arrive(index):
            pltpu.make_async_remote_copy(
                src_ref=block_at(index),
                dst_ref=block_at(index),
                send_sem=send_sem.at[0],
                recv_sem=recv_sem.at[index],
                device_id=device(o, i, 1 - c, head),
                device_id_type=MESH,
            ).wait_recv()

        sibling = device(o, i, 1 - c, head)
        i_peer = device(o, 1 - i, c, head)
        h_peer = device(o, i, c, 1 - head)
        order = []
        for d in range(1, outer // 2 + 1):
            order.append(d)
            if d != outer - d:
                order.append(outer - d)
        at = lambda d: lax.rem(o + d, outer)
        o_peers = [device(at(d), i, c, head) for d in order]
        peers = [sibling, i_peer, h_peer] + o_peers
        barrier = pltpu.get_barrier_semaphore()
        for peer in peers:
            pl.semaphore_signal(barrier, inc=1, device_id=peer, device_id_type=MESH)

        first_row = blk * tokens + head * slices
        own_pos = (
            span_ref[first_row // half_block] * half_block
            + first_row % half_block
            + lax.broadcasted_iota(jnp.int32, (slices, LANES), 0)
        )
        own = keys_in_ref[...].astype(jnp.float32)
        own_latent = own[:, :latent]
        own_latent = (
            own_latent
            * lax.rsqrt(jnp.mean(own_latent * own_latent, axis=1, keepdims=True) + norm_epsilon)
            * gain_ref[...]
        )
        cosine, sine = angles_of(own_pos, freq_ref[...], rope)
        own_rope = own[:, latent : latent + rope]
        own_rope = jnp.concatenate([own_rope] * (LANES // rope), axis=1)
        own_slot = slot(o, i, c, head)
        own_block = block_at(own_slot)
        own_block[:, :latent] = own_latent.astype(jnp.bfloat16)
        own_block[:, latent:] = rotate_tile(own_rope, cosine, sine, rope).astype(jnp.bfloat16)

        pl.semaphore_wait(barrier, len(peers))
        for peer in [i_peer, h_peer] + o_peers + [sibling]:
            send(own_slot, peer)
    else:
        keys_copy = pltpu.make_async_copy(keys_in_ref, keys_ref, load_sem.at[4])
        keys_copy.start()

    token = lax.broadcasted_iota(jnp.int32, (tokens, LANES), 0)
    query_pos = (
        jnp.where(token < half_block, span_ref[blk * 2], span_ref[blk * 2 + 1]) * half_block
        + token % half_block
    )
    key_lane = lax.broadcasted_iota(jnp.int32, (8, total), 1)
    key_half = key_lane // half_block
    key_span = jnp.zeros((8, total), jnp.int32)
    for entry in range(total // half_block):
        key_span = jnp.where(key_half == entry, span_ref[entry], key_span)
    key_pos = key_span * half_block + key_lane % half_block
    mask_ref[...] = jnp.where(key_pos[:1] <= query_pos[:, :1], 0.0, masked_score)
    cosine, sine = angles_of(query_pos, freq_ref[...], rope)
    loads[1].wait()
    per_tile = LANES // rope
    lane = lax.broadcasted_iota(jnp.int32, (tokens, LANES), 1)
    for tile in range(heads // per_tile):
        columns = rope_ref[:, tile * LANES : (tile + 1) * LANES].astype(jnp.float32)
        rotated = rotate_tile(columns, cosine, sine, rope)
        for part in range(per_tile):
            row = (tile * per_tile + part) * tokens
            query_ref[row : row + tokens, latent:] = jnp.where(
                lane // rope == part, rotated, 0.0
            ).astype(jnp.bfloat16)

    if remote:
        for d in order:
            index = slot(at(d), i, c, head)
            arrive(index)
            for peer in (i_peer, h_peer, sibling):
                send(index, peer)

    loads[0].wait()
    loads[2].wait()

    def lift(first, count):
        for h in range(first, first + count):
            query_ref[h * tokens : (h + 1) * tokens, :latent] = jnp.dot(
                nope_ref[:, h * nope : (h + 1) * nope],
                key_up_ref[h],
                preferred_element_type=jnp.float32,
            ).astype(jnp.bfloat16)

    if remote:
        steps = [0] + order
        per_step = -(-heads // len(steps))
        for n, d in enumerate(steps):
            lift(n * per_step, max(0, min(per_step, heads - n * per_step)))
            via_h, via_i = slot(at(d), i, c, 1 - head), slot(at(d), 1 - i, c, head)
            arrive(via_i)
            if d % 2 == 1:
                send(via_i, h_peer)
            send(via_i, sibling)
            arrive(via_h)
            if d % 2 == 0:
                send(via_h, i_peer)
            send(via_h, sibling)
        for d in steps:
            index = slot(at(d), 1 - i, c, 1 - head)
            arrive(index)
            send(index, sibling)
        for d in steps:
            for i_ in (i, 1 - i):
                for h_ in (head, 1 - head):
                    arrive(slot(at(d), i_, 1 - c, h_))
    else:
        lift(0, heads)
        keys_copy.wait()
    loads[3].wait()

    group = min(GROUP, heads)
    rows = group * tokens

    def attend(g, _):
        start = pl.multiple_of(g * rows, rows)
        scores = lax.dot_general(
            query_ref[pl.ds(start, rows), :],
            keys_ref[...],
            (((1,), (1,)), ((), ())),
            preferred_element_type=jnp.float32,
        )
        scores = scores.reshape(group, tokens, total) + mask_ref[...][None]
        top = jnp.max(scores, axis=2, keepdims=True)
        weight = jnp.exp2((scores - top) * scale)
        sums = jnp.sum(weight, axis=2, keepdims=True).reshape(rows, 1)
        product = jnp.dot(
            weight.reshape(rows, total).astype(jnp.bfloat16),
            keys_ref[:, :latent],
            preferred_element_type=jnp.float32,
        )
        lat_out = (product * (1.0 / sums)).astype(jnp.bfloat16)
        for n in range(group):
            column = pl.multiple_of((g * group + n) * value, value)
            out_ref[:, pl.ds(column, value)] = jnp.dot(
                lat_out[n * tokens : (n + 1) * tokens],
                value_up_ref[g * group + n],
                preferred_element_type=jnp.float32,
            ).astype(jnp.bfloat16)
        return 0

    lax.fori_loop(0, heads // group, attend, 0)
    store = pltpu.make_async_copy(out_ref, out_hbm, out_sem.at[0])
    store.start()
    for copy in sends:
        copy.wait_send()
    store.wait()


def shards(
    mesh, query_nope, query_rope, compressed, latent_gain, key_up, value_up, span_order
):
    tokens, (heads, nope, latent) = query_nope.shape[0], key_up.shape
    rope, value = query_rope.shape[1] // heads, value_up.shape[2]
    slices = compressed.shape[0]
    blocks, head_parts = mesh.shape["blk"], mesh.shape["head"]
    total = blocks * tokens
    half_block = tokens // 2
    half = rope // 2
    remote = head_parts == 2 and blocks % 4 == 0 and slices % 16 == 0 and half_block % slices == 0
    exponents = np.arange(LANES) % half
    freq = jnp.asarray((rope_base ** (-exponents / half)).astype(np.float32))[None]
    gain = latent_gain[None]
    if remote:
        keys_in = compressed
    else:
        rows = (
            lax.axis_index("blk") * tokens
            + lax.axis_index("head") * slices
            + jnp.arange(slices, dtype=jnp.int32)
        )
        pos = span_order[rows // half_block] * half_block + rows % half_block
        wide = compressed.astype(jnp.float32)
        lat = wide[:, :latent]
        lat = lat * lax.rsqrt(jnp.mean(lat * lat, axis=1, keepdims=True) + norm_epsilon) * gain
        angles = pos.astype(jnp.float32)[:, None] * freq[:, :half]
        a, b = wide[:, latent : latent + half], wide[:, latent + half :]
        cosine, sine = jnp.cos(angles), jnp.sin(angles)
        rot = [a * cosine - b * sine, a * sine + b * cosine]
        own = jnp.concatenate([lat] + rot * (LANES // rope), axis=1).astype(jnp.bfloat16)
        keys_in = lax.all_gather(own, ("blk", "head"), axis=0, tiled=True)
    any_space = pl.BlockSpec(memory_space=pl.ANY)
    vmem = pl.BlockSpec(memory_space=pltpu.VMEM)
    dims = (tokens, heads, nope, latent, rope, value, total, slices)
    return pl.pallas_call(
        functools.partial(body, dims, remote),
        out_shape=jax.ShapeDtypeStruct((tokens, heads * value), jnp.bfloat16),
        in_specs=[
            pl.BlockSpec(memory_space=pltpu.SMEM),
            vmem if remote else any_space,
            vmem,
            vmem,
            any_space,
            any_space,
            any_space,
            any_space,
        ],
        out_specs=any_space,
        scratch_shapes=[
            pltpu.VMEM(query_nope.shape, jnp.bfloat16),
            pltpu.VMEM(query_rope.shape, jnp.bfloat16),
            pltpu.VMEM(key_up.shape, jnp.bfloat16),
            pltpu.VMEM(value_up.shape, jnp.bfloat16),
            pltpu.VMEM((tokens, heads * value), jnp.bfloat16),
            pltpu.VMEM((total, latent + LANES), jnp.bfloat16),
            pltpu.VMEM((heads * tokens, latent + LANES), jnp.bfloat16),
            pltpu.VMEM((tokens, total), jnp.float32),
            pltpu.SemaphoreType.DMA((5,)),
            pltpu.SemaphoreType.DMA((1,)),
            pltpu.SemaphoreType.DMA((2 * blocks if remote else 1,)),
            pltpu.SemaphoreType.DMA((2 * blocks if remote else 1,)),
        ],
        compiler_params=pltpu.CompilerParams(
            vmem_limit_bytes=60 * 1024 * 1024,
            has_side_effects=remote,
            **({"collective_id": 0} if remote else {}),
        ),
    )(span_order, keys_in, gain, freq, query_nope, query_rope, key_up, value_up)


def solution(mesh):
    in_specs = (
        P("blk", "head"),
        P("blk", "head"),
        P(("blk", "head"), None),
        P(),
        P("head", None, None),
        P("head", None, None),
        P(),
    )
    return jax.shard_map(
        functools.partial(shards, mesh),
        mesh=mesh,
        in_specs=in_specs,
        out_specs=P("blk", "head"),
        check_vma=False,
    )
```

time: 78.4 us -> 30 us (0.38)
  waiting for transfers between devices: 34.5 us -> 0 us
  Pallas kernels: 0 us -> 27.9 us
  between operations: 13.6 us -> 0.01 us
  matrix products: 11.6 us -> 0 us
  other arithmetic: 9.23 us -> 0 us
  blocking collectives: 4.17 us -> 0 us
  local copies, waits for them, and re-layouts: 4.67 us -> 1.87 us
    all_gather x1 -> x0, waiting for transfers between devices: 34.5 us -> none  [shards(): shard_keys = lax.all_gather(block_keys, 'blk', axis=0, tiled=True)]
    pallas_call x0 -> x1, Pallas kernels: none -> 27.9 us  [shards(): pl.pallas_call(functools.partial(body, dims, remote), out_shape=jax.Shape...]
    dot_general x4 -> x0, matrix products: 11.6 us -> none  [the longest x1 4.93 us: shards(): jnp.einsum('qd,kd->qk', queries, shard_keys, preferred_element_type=jnp.f...]
    reduce_sum x5 -> x0, other arithmetic: 5.45 us -> none  [the longest x1 2.85 us: shards(): new_sum = jnp.sum(weight, axis=1)]
    all_gather x1 -> x0, blocking collectives: 4.17 us -> none  [shards(): block_keys = lax.all_gather(key_rows, 'head', axis=0, tiled=True)]
    convert_element_type x4 -> x0, other arithmetic: 1.59 us -> none  [the longest x1 0.86 us: shards(): latent = latent.astype(jnp.bfloat16)]
    concatenate x1 -> x0, local copies, waits for them, and re-layouts: 1.5 us -> none  [shards(): jnp.concatenate([query_lat, query_rot], axis=2)]
    unnamed x10 -> x1, local copies, waits for them, and re-layouts: 0.4 us -> 1.87 us
  transfers between devices with their start and end apart: 1 -> 0, of which waited for: 1 -> 0; matrix products, arithmetic and copies ran while one was open for 9% -> 0% of each run, Pallas kernels for 0% -> 0%
where the time goes in v1:
time: 30 us; the launch traced here: 29.8 us
  Pallas kernels  27.9 us (93%)
  local copies, waits for them, and re-layouts  1.87 us (6%)
    pallas_call x1, Pallas kernels, shards(): pl.pallas_call(functools.partial(body, dims, remote), out_shape=jax.Shape...  27.9 us
    unnamed x1, local copies, waits for them, and re-layouts  1.87 us

profile of v1, /device:TPU:1, one launch (start us, length us, event | category | flops | bytes accessed | tf_op | source)
XLA Modules:
  0.0 29.8 jit_solution(17287209826241875678)
XLA Ops:
  0.0 27.9 %shard_map.82 = bf16[64,4096]{1,0:T(8,128)(2,1)} custom-call(s32[32]{0:T(128)} %span_ref.1, bf16[32,576]{1,0:T(8,128)(2,1)} %keys_in_ref.1, f32[1,512]{1,0:T(1,128)} %bitcast.1, f32[1,128]{1,0:T(1,128)} %constant.3.freq_ref, bf16[64,4096]{1,0:T(8,128)(2,1)} %nope_hbm.1, bf16[64,2048]{1,0:T(8,128)(2,1)} %rope_hbm.1, bf16[32,128,512]{2,1,0:T(8,128)(2,1)} %key_up_hbm.1, ...), custom_call_target="tpu_custom_call" | custom-call | tf_op jit(solution)/shard_map/pallas_call | solution.py:300
  27.9 1.9 %copy.10 = bf16[64,4096]{1,0:T(8,128)(2,1)} copy(bf16[64,4096]{1,0:T(8,128)(2,1)} %shard_map.82) | data formatting | bytes 1048576
